TPU v7x, 32 devices: a whole 2x2x4 slice. The times are simulated.
32 devices in a mesh: head: 8 (over z, core), kv: 4 (over y, x).
Axes of the slice: x: 2, y: 2, z: 4, core: 2. Of those that a mesh axis runs over, the one named last changes fastest.
Arguments:
- queries: bfloat16 [2048, 8192], P(('kv', 'head')), may hold values from -6 to 6
- key_rows: bfloat16 [2048, 1024], P(('kv', 'head')), may hold values from -6 to 6
- value_matrix: bfloat16 [2048, 1024], P(('kv', 'head')), may hold values from -6 to 6
- doc_ids: int32 [2048], P(('kv', 'head')), may hold values from 0 to 5, as said below
Outputs:
- attended: bfloat16 [2048, 8192], P(('kv', 'head'))
Inputs may be any that keep to these rules, and one draw needn't show every extreme that they name: doc_ids starts at 0, never falls, and rises by one at the first token of each of the 6 documents; every document starts at an even position and has 2 tokens or more.
All inputs are finite; a program needn't handle non-finite values.
Results may differ from a plain program's by a relative error of at most 0.015.
Values may be sent and summed in bfloat16 or wider, within the bound.
A program may use at most 64 MiB of HBM per device.

v0:
```python
import math
import jax
import jax.numpy as jnp
from jax import lax
from jax.sharding import PartitionSpec as P

QUERY_HEADS = 64
KEY_VALUE_HEADS = 8
HEAD_SIZE = 128
NEG_FILL = -1e30


def repeat_heads(input_matrix, head_repeats):
    row_number = input_matrix.shape[0]
    heads_apart = input_matrix.reshape(row_number, KEY_VALUE_HEADS, 1, HEAD_SIZE)
    expanded_heads = jnp.broadcast_to(
        heads_apart, (row_number, KEY_VALUE_HEADS, head_repeats, HEAD_SIZE)
    )
    return expanded_heads.reshape(row_number, KEY_VALUE_HEADS * head_repeats * HEAD_SIZE)


def block_terms(query_group, query_pos, query_doc, key_block, value_block, key_pos, key_doc):
    key_count = key_block.shape[0]
    key_value_slot = query_group.shape[1]
    key_heads = key_block.reshape(key_count, key_value_slot, HEAD_SIZE)
    value_heads = value_block.reshape(key_count, key_value_slot, HEAD_SIZE)
    scores = jnp.einsum(
        "rkgd,ckd->kgrc", query_group, key_heads, preferred_element_type=jnp.float32
    ) * HEAD_SIZE ** (-0.5)
    allowed = (key_pos[None, :] <= query_pos[:, None]) & (key_doc[None, :] == query_doc[:, None])
    masked = jnp.where(allowed, scores, NEG_FILL)
    row_peak = jnp.max(masked, axis=-1)
    weights = jnp.where(allowed, jnp.exp(masked - row_peak[..., None]), 0.0)
    row_total = jnp.sum(weights, axis=-1)
    weighted = jnp.einsum(
        "kgrc,ckd->kgrd",
        weights.astype(jnp.bfloat16),
        value_heads,
        preferred_element_type=jnp.float32,
    )
    return (row_peak, row_total, weighted)


def attend_block(query_group, query_pos, query_doc, key_block, value_block, key_pos, key_doc):
    return block_terms(query_group, query_pos, query_doc, key_block, value_block, key_pos, key_doc)


def combine_terms(first_terms, second_terms):
    joint_peak = jnp.maximum(first_terms[0], second_terms[0])
    left_factor = jnp.exp(first_terms[0] - joint_peak)
    right_factor = jnp.exp(second_terms[0] - joint_peak)
    joint_total = first_terms[1] * left_factor + second_terms[1] * right_factor
    joint_weighted = (
        first_terms[2] * left_factor[..., None] + second_terms[2] * right_factor[..., None]
    )
    return (joint_peak, joint_total, joint_weighted)


def local(queries, key_rows, value_matrix, doc_ids):
    head_number = lax.axis_size("head")
    head_repeats = max(1, head_number // KEY_VALUE_HEADS)
    key_send = repeat_heads(key_rows, head_repeats)
    value_send = repeat_heads(value_matrix, head_repeats)
    query_block, key_block, value_block = (
        lax.all_to_all(queries, "head", split_axis=1, concat_axis=0, tiled=True),
        lax.all_to_all(key_send, "head", split_axis=1, concat_axis=0, tiled=True),
        lax.all_to_all(value_send, "head", split_axis=1, concat_axis=0, tiled=True),
    )
    block_len = query_block.shape[0]
    doc_global = lax.all_gather(doc_ids, ("kv", "head"), axis=0, tiled=True)
    query_width = query_block.shape[1]
    present_heads = query_width // HEAD_SIZE
    key_value_slot = max(1, present_heads // (QUERY_HEADS // KEY_VALUE_HEADS))
    group_here = present_heads // key_value_slot
    own_first = lax.axis_index("kv") * block_len
    own_pos = own_first + jnp.arange(block_len, dtype=jnp.int32)
    own_doc = jnp.take(doc_global, own_pos)
    query_group = query_block.reshape(block_len, key_value_slot, group_here, HEAD_SIZE)
    term_shape = (key_value_slot, group_here, block_len)
    initial = (
        jnp.full(term_shape, NEG_FILL, jnp.float32),
        jnp.zeros(term_shape, jnp.float32),
        jnp.zeros(term_shape + (HEAD_SIZE,), jnp.float32),
    )
    key_piece = lax.all_gather(key_block, "kv", axis=0, tiled=True)
    value_piece = lax.all_gather(value_block, "kv", axis=0, tiled=True)
    piece_rows = key_piece.shape[0]
    step_rows = math.gcd(piece_rows, 1024)

    def one_step(step_index, inner):
        local_first = step_index * step_rows
        keys_now = lax.dynamic_slice_in_dim(key_piece, local_first, step_rows, 0)
        values_now = lax.dynamic_slice_in_dim(value_piece, local_first, step_rows, 0)
        key_pos = local_first + jnp.arange(step_rows, dtype=jnp.int32)
        key_doc = jnp.take(doc_global, key_pos)
        return combine_terms(
            inner,
            attend_block(query_group, own_pos, own_doc, keys_now, values_now, key_pos, key_doc),
        )

    folded = lax.fori_loop(0, piece_rows // step_rows, one_step, initial)
    result = (
        (folded[2] / folded[1][..., None]).transpose(2, 0, 1, 3).reshape(block_len, query_width)
    )
    result = result.astype(jnp.bfloat16)
    return lax.all_to_all(result, "head", split_axis=0, concat_axis=1, tiled=True)


def solution(mesh):
    return jax.shard_map(
        local,
        mesh=mesh,
        in_specs=(
            P(("kv", "head"), None),
            P(("kv", "head"), None),
            P(("kv", "head"), None),
            P(("kv", "head")),
        ),
        out_specs=P(("kv", "head"), None),
        check_vma=False,
    )
```

profile of v0, /device:TPU:0, one launch (start us, length us, event | category | flops | bytes accessed | tf_op | source)
XLA Modules:
  0.0 176.7 jit_solution(10033229204570758715)
XLA Ops:
  0.0 0.0 copy-start
  0.0 0.9 copy-done
  0.9 0.7 copy_bitcast_fusion.2
  1.6 6.4 %all-to-all-start = ((bf16[64,8,128]{2,0,1:T(8,128)(2,1)}), bf16[64,8,128]{2,0,1:T(8,128)(2,1)S(1)}, u32[]{:S(2)}, u32[]{:S(2)}) async-start(bf16[64,8,128]{2,0,1:T(8,128)(2,1)} %copy_bitcast_fusion.2), calls=%async_computation | async-start | bytes 262144 | tf_op jit(solution)/shard_map/all_to_all | solution.py:66
  7.9 1.6 copy_bitcast_fusion.1
  9.5 5.2 %all-to-all-done = bf16[64,8,128]{2,0,1:T(8,128)(2,1)S(1)} async-done(((bf16[64,8,128]{2,0,1:T(8,128)(2,1)}), bf16[64,8,128]{2,0,1:T(8,128)(2,1)S(1)}, u32[]{:S(2)}, u32[]{:S(2)}) %all-to-all-start) | async-done | bytes 131104 | tf_op jit(solution)/shard_map/all_to_all | solution.py:66
  14.7 3.4 %all-to-all-start.2 = ((bf16[64,8,128]{2,0,1:T(8,128)(2,1)}), bf16[64,8,128]{2,0,1:T(8,128)(2,1)S(1)}, u32[]{:S(2)}, u32[]{:S(2)}) async-start(bf16[64,8,128]{2,0,1:T(8,128)(2,1)} %copy_bitcast_fusion.1), calls=%async_computation.2 | async-start | bytes 262144 | tf_op jit(solution)/shard_map/all_to_all | solution.py:67
  18.1 2.3 %copy.30 = bf16[8,8,8,1024]{3,2,0,1:T(8,128)(2,1)} copy(bf16[8,8,8,1024]{3,2,1,0:T(8,128)(2,1)} %bitcast.121) | data formatting | bytes 2097152 | tf_op jit(solution)/shard_map/all_to_all | solution.py:65
  20.4 4.4 %all-to-all-done.2 = bf16[64,8,128]{2,0,1:T(8,128)(2,1)S(1)} async-done(((bf16[64,8,128]{2,0,1:T(8,128)(2,1)}), bf16[64,8,128]{2,0,1:T(8,128)(2,1)S(1)}, u32[]{:S(2)}, u32[]{:S(2)}) %all-to-all-start.2) | async-done | bytes 131104 | tf_op jit(solution)/shard_map/all_to_all | solution.py:67
  24.8 3.6 %all-to-all-start.1 = ((bf16[64,8,1024]{2,0,1:T(8,128)(2,1)}), bf16[64,8,1024]{2,0,1:T(8,128)(2,1)S(1)}, u32[]{:S(2)}, u32[]{:S(2)}) async-start(bf16[64,8,1024]{2,0,1:T(8,128)(2,1)} %bitcast.93), calls=%async_computation.1 | async-start | bytes 2097152 | tf_op jit(solution)/shard_map/all_to_all | solution.py:65
  28.4 1.3 dynamic-slice
  30.4 0.9 dynamic-update-slice
  31.2 43.9 %all-reduce = s32[2048]{0:T(1024)S(1)} all-reduce(s32[2048]{0:T(1024)S(1)} %dynamic-update-slice), channel_id=1, replica_groups=mesh['head'=8,'kv'=4] {'kv','head'}, use_global_device_ids=true, to_apply=%add | all-reduce | flops 2048 | bytes 16384
  75.2 3.1 %gather_fusion.1 = s32[512]{0:T(512)S(1)} fusion(s32[2048]{0:T(1024)S(1)} %all-reduce, s32[1024]{0:T(1024)S(1)} %pad_clamp_fusion), kind=kCustom, calls=%fused_computation.1 | custom fusion | bytes 6144 | tf_op jit(solution)/shard_map/jit(_take)/gather | solution.py:77
  78.3 11.6 %all_gather.11 = bf16[2048,128]{1,0:T(8,128)(2,1)S(1)} all-gather(bf16[512,128]{1,0:T(8,128)(2,1)S(1)} %bitcast.124), channel_id=1, replica_groups=mesh['head'=8,'kv'=4] {'kv'}, dimensions={0}, use_global_device_ids=true | all-gather | bytes 655360 | tf_op jit(solution)/shard_map/all_gather | solution.py:86
  89.9 9.0 %all_gather.10 = bf16[2048,128]{1,0:T(8,128)(2,1)S(1)} all-gather(bf16[512,128]{1,0:T(8,128)(2,1)S(1)} %bitcast.123), channel_id=1, replica_groups=mesh['head'=8,'kv'=4] {'kv'}, dimensions={0}, use_global_device_ids=true | all-gather | bytes 655360 | tf_op jit(solution)/shard_map/all_gather | solution.py:85
  98.9 0.0 all-to-all-done.1
  98.9 0.3 copy.26
  99.2 0.1 copy.18
  99.3 43.2 %while.18 = (s32[]{:T(128)}, f32[1,8,512]{2,1,0:T(8,128)S(1)}, f32[1,8,512]{2,1,0:T(8,128)S(1)}, f32[1,8,512,128]{3,2,1,0:T(8,128)}, s32[2048]{0:T(1024)S(1)}, /...) while((s32[]{:T(128)}, f32[1,8,512]{2,1,0:T(8,128)S(1)}, ...), condition=%wide.region_3.4_spmd.clone, body=%wide.region_0.3_spmd.clone.sunk | while | flops 2205726208 | bytes 75335952 | solution.py:101
  99.4 6.2 %gather_fusion = s32[1024]{0:T(1024)S(1)} fusion(s32[2048]{0:T(1024)S(1)} %get-tuple-element.370, s32[1024]{0:T(1024)S(1)} %broadcast_clamp_fusion.2), kind=kCustom, calls=%fused_computation.clone.clone.1 | custom fusion | bytes 12288 | tf_op jit(solution)/shard_map/while/body/eval_jaxpr/jit(_take)/gather | solution.py:95
  105.6 0.8 compare_and_fusion.2
  106.4 2.9 %fusion.41 = (f32[8,512]{1,0:T(8,128)S(1)}, f32[1024,512,8]{1,0,2:T(8,128)S(1)}) fusion(pred[512,1024]{0,1:T(8,128)(4,1)S(1)} %compare_and_fusion.2, bf16[512,1,8,128]{3,0,2,1:T(8,128)(2,1)S(1)} %get-tuple-element.373, bf16[2048,128]{1,0:T(8,128)(2,1)S(1)} %get-tuple-element.372, s32[]{:T(128)S(6)} %select_n.145), kind=kOutput, calls=%fused_computation.5.clone.1 | convolution fusion | flops 1086320640 | bytes 18628612 | tf_op jit(solution)/shard_map/while/body/eval_jaxpr/rkgd,ckd->kgrc/dot_general | solution.py:27
  109.3 0.0 copy-start.1
  109.3 4.0 %fusion.43 = f32[8,512]{1,0:T(8,128)S(1)} fusion(f32[1024,512,8]{1,0,2:T(8,128)S(1)} %get-tuple-element.334, f32[8,512]{1,0:T(8,128)S(1)} %get-tuple-element.332, pred[512,1024]{0,1:T(8,128)(4,1)S(1)} %compare_and_fusion.2), kind=kLoop, calls=%fused_computation.7.clone.1 | loop fusion | flops 20967424 | bytes 17334272 | tf_op jit(solution)/shard_map/while/body/eval_jaxpr/reduce_sum | solution.py:34
  113.4 0.0 copy-done.1
  113.4 6.1 %bitcast_add_fusion.2 = f32[1,8,512,128]{3,2,1,0:T(8,128)S(1)} fusion(f32[1,8,512,128]{3,2,1,0:T(8,128)S(1)} %copy-done.1, f32[1024,512,8]{1,0,2:T(8,128)S(1)} %get-tuple-element.334, f32[8,512]{1,0:T(8,128)S(1)} %get-tuple-element.332, pred[512,1024]{0,1:T(8,128)(4,1)S(1)} %compare_and_fusion.2, f32[8,512]{1,0:T(8,128)S(1)} %get-tuple-element.336, ...), kind=kOutput, calls=%fused_computation.11.clone.1 | convolution fusion | flops 1096810496 | bytes 21807108 | tf_op jit(solution)/shard_map/while/body/eval_jaxpr/kgrc,ckd->kgrd/dot_general | solution.py:35
  119.6 0.0 copy-start.2
  119.6 1.3 copy-done.2
  120.9 6.2 %gather_fusion = s32[1024]{0:T(1024)S(1)} fusion(s32[2048]{0:T(1024)S(1)} %get-tuple-element.370, s32[1024]{0:T(1024)S(1)} %broadcast_clamp_fusion.2), kind=kCustom, calls=%fused_computation.clone.clone.1 | custom fusion | bytes 12288 | tf_op jit(solution)/shard_map/while/body/eval_jaxpr/jit(_take)/gather | solution.py:95
  127.1 0.8 compare_and_fusion.2
  128.0 2.9 %fusion.41 = (f32[8,512]{1,0:T(8,128)S(1)}, f32[1024,512,8]{1,0,2:T(8,128)S(1)}) fusion(pred[512,1024]{0,1:T(8,128)(4,1)S(1)} %compare_and_fusion.2, bf16[512,1,8,128]{3,0,2,1:T(8,128)(2,1)S(1)} %get-tuple-element.373, bf16[2048,128]{1,0:T(8,128)(2,1)S(1)} %get-tuple-element.372, s32[]{:T(128)S(6)} %select_n.145), kind=kOutput, calls=%fused_computation.5.clone.1 | convolution fusion | flops 1086320640 | bytes 18628612 | tf_op jit(solution)/shard_map/while/body/eval_jaxpr/rkgd,ckd->kgrc/dot_general | solution.py:27
  130.9 0.0 copy-start.1
  130.9 4.0 %fusion.43 = f32[8,512]{1,0:T(8,128)S(1)} fusion(f32[1024,512,8]{1,0,2:T(8,128)S(1)} %get-tuple-element.334, f32[8,512]{1,0:T(8,128)S(1)} %get-tuple-element.332, pred[512,1024]{0,1:T(8,128)(4,1)S(1)} %compare_and_fusion.2), kind=kLoop, calls=%fused_computation.7.clone.1 | loop fusion | flops 20967424 | bytes 17334272 | tf_op jit(solution)/shard_map/while/body/eval_jaxpr/reduce_sum | solution.py:34
  135.0 0.0 copy-done.1
  135.0 6.1 %bitcast_add_fusion.2 = f32[1,8,512,128]{3,2,1,0:T(8,128)S(1)} fusion(f32[1,8,512,128]{3,2,1,0:T(8,128)S(1)} %copy-done.1, f32[1024,512,8]{1,0,2:T(8,128)S(1)} %get-tuple-element.334, f32[8,512]{1,0:T(8,128)S(1)} %get-tuple-element.332, pred[512,1024]{0,1:T(8,128)(4,1)S(1)} %compare_and_fusion.2, f32[8,512]{1,0:T(8,128)S(1)} %get-tuple-element.336, ...), kind=kOutput, calls=%fused_computation.11.clone.1 | convolution fusion | flops 1096810496 | bytes 21807108 | tf_op jit(solution)/shard_map/while/body/eval_jaxpr/kgrc,ckd->kgrd/dot_general | solution.py:35
  141.1 0.0 copy-start.2
  141.2 1.3 copy-done.2
  142.5 2.0 %fusion.26 = bf16[512,1,8,128]{3,0,2,1:T(8,128)(2,1)S(1)} fusion(f32[1,8,512,128]{3,2,1,0:T(8,128)} %get-tuple-element.175, f32[8,512]{1,0:T(8,128)S(1)} %bitcast.122), kind=kLoop, calls=%fused_computation.42 | loop fusion | flops 1048576 | bytes 3162112 | tf_op jit(solution)/shard_map/convert_element_type | solution.py:105
  144.4 0.7 copy.19
  145.1 0.5 convert_element_type.19
  145.6 30.0 %all_to_all.70 = bf16[8,64,1024]{2,1,0:T(8,128)(2,1)S(1)} all-to-all(bf16[8,64,1024]{2,1,0:T(8,128)(2,1)S(1)} %convert_element_type.19), channel_id=1, replica_groups=mesh['head'=8,'kv'=4] {'head'}, dimensions={0} | all-to-all | bytes 2097152 | tf_op jit(solution)/shard_map/all_to_all | solution.py:106
  175.6 1.1 copy.25
  (21 shorter events, 0.2 us)
Async XLA Ops:
  0.0 0.9 copy-start
  1.6 13.1 %all-to-all-start = ((bf16[64,8,128]{2,0,1:T(8,128)(2,1)}), bf16[64,8,128]{2,0,1:T(8,128)(2,1)S(1)}, u32[]{:S(2)}, u32[]{:S(2)}) async-start(bf16[64,8,128]{2,0,1:T(8,128)(2,1)} %copy_bitcast_fusion.2), calls=%async_computation | async-start | bytes 262144 | tf_op jit(solution)/shard_map/all_to_all | solution.py:66
  14.7 10.1 %all-to-all-start.2 = ((bf16[64,8,128]{2,0,1:T(8,128)(2,1)}), bf16[64,8,128]{2,0,1:T(8,128)(2,1)S(1)}, u32[]{:S(2)}, u32[]{:S(2)}) async-start(bf16[64,8,128]{2,0,1:T(8,128)(2,1)} %copy_bitcast_fusion.1), calls=%async_computation.2 | async-start | bytes 262144 | tf_op jit(solution)/shard_map/all_to_all | solution.py:67
  24.8 74.1 %all-to-all-start.1 = ((bf16[64,8,1024]{2,0,1:T(8,128)(2,1)}), bf16[64,8,1024]{2,0,1:T(8,128)(2,1)S(1)}, u32[]{:S(2)}, u32[]{:S(2)}) async-start(bf16[64,8,1024]{2,0,1:T(8,128)(2,1)} %bitcast.93), calls=%async_computation.1 | async-start | bytes 2097152 | tf_op jit(solution)/shard_map/all_to_all | solution.py:65
  109.3 4.1 %copy-start.1 = (f32[1,8,512,128]{3,2,1,0:T(8,128)S(1)}, f32[1,8,512,128]{3,2,1,0:T(8,128)}, u32[]{:S(2)}) copy-start(f32[1,8,512,128]{3,2,1,0:T(8,128)} %get-tuple-element.355) | copy-start | bytes 6291460 | tf_op jit(solution)/shard_map/while
  119.6 1.3 copy-start.2
  130.9 4.1 %copy-start.1 = (f32[1,8,512,128]{3,2,1,0:T(8,128)S(1)}, f32[1,8,512,128]{3,2,1,0:T(8,128)}, u32[]{:S(2)}) copy-start(f32[1,8,512,128]{3,2,1,0:T(8,128)} %get-tuple-element.355) | copy-start | bytes 6291460 | tf_op jit(solution)/shard_map/while
  141.1 1.3 copy-start.2
where the time goes:
time: 177 us
  blocking collectives  94.4 us (53%)
  local copies, waits for them, and re-layouts  28.4 us (16%)
  matrix products  18.1 us (10%)
  starting transfers between devices  13.3 us (8%)
  other arithmetic  11.8 us (7%)
  waiting for transfers between devices  9.58 us (5%)
    unnamed x1, blocking collectives  43.9 us
    all_to_all x1, blocking collectives, local(): lax.all_to_all(result, 'head', split_axis=0, concat_axis=1, tiled=True)  30 us
    gather x2, local copies, waits for them, and re-layouts, one_step(): key_doc = jnp.take(doc_global, key_pos)  12.3 us
    dot_general x2, matrix products, block_terms(): jnp.einsum('kgrc,ckd->kgrd', weights.astype(jnp.bfloat16), value_heads, p...  12.3 us
    all_gather x1, blocking collectives, local(): value_piece = lax.all_gather(value_block, 'kv', axis=0, tiled=True)  11.6 us
    all_gather x1, blocking collectives, local(): key_piece = lax.all_gather(key_block, 'kv', axis=0, tiled=True)  9 us
    reduce_sum x2, other arithmetic, block_terms(): row_total = jnp.sum(weights, axis=-1)  8.05 us
    all_to_all x1, starting transfers between devices, local(): lax.all_to_all(key_send, 'head', split_axis=1, concat_axis=0, tiled=True)  6.35 us
  transfers between devices with their start and end apart: 3, of which 2 were waited for; matrix products, arithmetic and copies ran while one was open for 5% of the time, Pallas kernels for 0%

commit v1 on v0

--- a/solution.py
+++ b/solution.py
@@ -64,7 +64,12 @@
     query_block, key_block, value_block = (
         lax.all_to_all(queries, "head", split_axis=1, concat_axis=0, tiled=True),
         lax.all_to_all(key_send, "head", split_axis=1, concat_axis=0, tiled=True),
-        lax.all_to_all(value_send, "head", split_axis=1, concat_axis=0, tiled=True),
+        jnp.concatenate(
+            lax.all_to_all(
+                jnp.stack(jnp.split(value_send, lax.axis_size("head"), axis=1)), "head", 0, 0
+            ),
+            axis=0,
+        ),
     )
     block_len = query_block.shape[0]
     doc_global = lax.all_gather(doc_ids, ("kv", "head"), axis=0, tiled=True)

time: 177 us -> 183 us (1.034)
  local copies, waits for them, and re-layouts: 28.4 us -> 34.6 us
  waiting for transfers between devices: 9.58 us -> 4.47 us
  matrix products: 18.1 us -> 20.2 us
    unnamed x7 -> x14, local copies, waits for them, and re-layouts: 3.49 us -> 12.6 us
    all_to_all x1, waiting for transfers between devices: 5.18 us -> 0.01 us  [local(): lax.all_to_all(key_send, 'head', split_axis=1, concat_axis=0, tiled=True)]
    while x10 -> x2, local copies, waits for them, and re-layouts: 2.68 us -> 0.01 us
    dot_general x2, matrix products: 12.3 us -> 14.4 us  [block_terms(): jnp.einsum('kgrc,ckd->kgrd', weights.astype(jnp.bfloat16), value_heads, p...]
  transfers between devices with their start and end apart: 3 -> 3, of which waited for: 2 -> 1; matrix products, arithmetic and copies ran while one was open for 5% -> 10% of each run, Pallas kernels for 0% -> 0%
where the time goes in v1:
time: 183 us; the launch traced here: 182 us
  blocking collectives  94.6 us (52%)
  local copies, waits for them, and re-layouts  34.6 us (19%)
  matrix products  20.2 us (11%)
  starting transfers between devices  15 us (8%)
  other arithmetic  11.8 us (6%)
  waiting for transfers between devices  4.47 us (2%)
    unnamed x1, blocking collectives  44.1 us
    all_to_all x1, blocking collectives, local(): lax.all_to_all(result, 'head', split_axis=0, concat_axis=1, tiled=True)  30 us
    dot_general x2, matrix products, block_terms(): jnp.einsum('kgrc,ckd->kgrd', weights.astype(jnp.bfloat16), value_heads, p...  14.4 us
    unnamed x14, local copies, waits for them, and re-layouts  12.6 us
    gather x2, local copies, waits for them, and re-layouts, one_step(): key_doc = jnp.take(doc_global, key_pos)  12.3 us
    all_gather x1, blocking collectives, local(): value_piece = lax.all_gather(value_block, 'kv', axis=0, tiled=True)  11.6 us
    all_gather x1, blocking collectives, local(): key_piece = lax.all_gather(key_block, 'kv', axis=0, tiled=True)  9 us
    reduce_sum x2, other arithmetic, block_terms(): row_total = jnp.sum(weights, axis=-1)  8.05 us
  transfers between devices with their start and end apart: 3, of which 1 were waited for; matrix products, arithmetic and copies ran while one was open for 10% of the time, Pallas kernels for 0%

profile of v1, /device:TPU:0, one launch (start us, length us, event | category | flops | bytes accessed | tf_op | source)
XLA Modules:
  0.0 181.6 jit_solution(3909484319638333116)
XLA Ops:
  0.0 0.0 copy-start
  0.0 0.9 copy-done
  0.9 0.7 copy_bitcast_fusion.1
  1.6 6.4 %all-to-all-start = ((bf16[64,8,128]{2,0,1:T(8,128)(2,1)}), bf16[64,8,128]{2,0,1:T(8,128)(2,1)S(1)}, u32[]{:S(2)}, u32[]{:S(2)}) async-start(bf16[64,8,128]{2,0,1:T(8,128)(2,1)} %copy_bitcast_fusion.1), calls=%async_computation | async-start | bytes 262144 | tf_op jit(solution)/shard_map/all_to_all | solution.py:66
  7.9 1.3 constant_dynamic-update-slice_fusion.7
  9.3 1.3 constant_dynamic-update-slice_fusion.6
  10.6 1.3 constant_dynamic-update-slice_fusion.5
  11.9 1.3 constant_dynamic-update-slice_fusion.4
  13.2 1.3 constant_dynamic-update-slice_fusion.3
  14.5 1.3 constant_dynamic-update-slice_fusion.2
  15.8 1.3 constant_dynamic-update-slice_fusion.1
  17.2 1.3 constant_dynamic-update-slice_fusion
  18.5 0.0 all-to-all-done
  18.5 5.1 %all-to-all-start.2 = ((bf16[8,64,128]{2,1,0:T(8,128)(2,1)}), bf16[8,64,128]{2,1,0:T(8,128)(2,1)S(1)}, u32[]{:S(2)}, u32[]{:S(2)}) async-start(bf16[8,64,128]{2,1,0:T(8,128)(2,1)} %constant_dynamic-update-slice_fusion), calls=%async_computation.2 | async-start | bytes 262144 | tf_op jit(solution)/shard_map/all_to_all | solution.py:68
  23.6 2.3 %copy.25 = bf16[8,8,8,1024]{3,2,0,1:T(8,128)(2,1)} copy(bf16[8,8,8,1024]{3,2,1,0:T(8,128)(2,1)} %bitcast.130) | data formatting | bytes 2097152 | tf_op jit(solution)/shard_map/all_to_all | solution.py:65
  25.9 4.5 %all-to-all-done.2 = bf16[8,64,128]{2,1,0:T(8,128)(2,1)S(1)} async-done(((bf16[8,64,128]{2,1,0:T(8,128)(2,1)}), bf16[8,64,128]{2,1,0:T(8,128)(2,1)S(1)}, u32[]{:S(2)}, u32[]{:S(2)}) %all-to-all-start.2) | async-done | bytes 131104 | tf_op jit(solution)/shard_map/all_to_all | solution.py:68
  30.3 3.6 %all-to-all-start.1 = ((bf16[64,8,1024]{2,0,1:T(8,128)(2,1)}), bf16[64,8,1024]{2,0,1:T(8,128)(2,1)S(1)}, u32[]{:S(2)}, u32[]{:S(2)}) async-start(bf16[64,8,1024]{2,0,1:T(8,128)(2,1)} %bitcast.102), calls=%async_computation.1 | async-start | bytes 2097152 | tf_op jit(solution)/shard_map/all_to_all | solution.py:65
  33.9 1.2 dynamic-slice
  35.8 0.9 dynamic-update-slice
  36.6 44.1 %all-reduce = s32[2048]{0:T(1024)S(1)} all-reduce(s32[2048]{0:T(1024)S(1)} %dynamic-update-slice), channel_id=1, replica_groups=mesh['head'=8,'kv'=4] {'kv','head'}, use_global_device_ids=true, to_apply=%add | all-reduce | flops 2048 | bytes 16384
  80.7 3.1 %gather_fusion.1 = s32[512]{0:T(512)S(1)} fusion(s32[2048]{0:T(1024)S(1)} %all-reduce, s32[1024]{0:T(1024)S(1)} %pad_clamp_fusion), kind=kCustom, calls=%fused_computation.1 | custom fusion | bytes 6144 | tf_op jit(solution)/shard_map/jit(_take)/gather | solution.py:82
  83.9 11.6 %all_gather.11 = bf16[2048,128]{1,0:T(8,128)(2,1)S(1)} all-gather(bf16[512,128]{1,0:T(8,128)(2,1)S(1)} %bitcast.133), channel_id=1, replica_groups=mesh['head'=8,'kv'=4] {'kv'}, dimensions={0}, use_global_device_ids=true | all-gather | bytes 655360 | tf_op jit(solution)/shard_map/all_gather | solution.py:91
  95.5 9.0 %all_gather.10 = bf16[2048,128]{1,0:T(8,128)(2,1)S(1)} all-gather(bf16[512,128]{1,0:T(8,128)(2,1)S(1)} %bitcast.132), channel_id=1, replica_groups=mesh['head'=8,'kv'=4] {'kv'}, dimensions={0}, use_global_device_ids=true | all-gather | bytes 655360 | tf_op jit(solution)/shard_map/all_gather | solution.py:90
  104.5 0.0 all-to-all-done.1
  104.5 0.3 copy.22
  104.8 0.1 copy.15
  104.9 42.6 %while.18 = (s32[]{:T(128)}, f32[1,8,512]{2,1,0:T(8,128)S(1)}, f32[1,8,512]{2,1,0:T(8,128)S(1)}, f32[1,8,512,128]{3,2,1,0:T(8,128)}, s32[2048]{0:T(1024)S(1)}, /...) while((s32[]{:T(128)}, f32[1,8,512]{2,1,0:T(8,128)S(1)}, ...), condition=%wide.region_3.4_spmd.clone, body=%wide.region_0.3_spmd.clone.sunk | while | flops 2205726208 | bytes 58558680 | solution.py:106
  105.0 6.2 %gather_fusion = s32[1024]{0:T(1024)S(1)} fusion(s32[2048]{0:T(1024)S(1)} %get-tuple-element.370, s32[1024]{0:T(1024)S(1)} %broadcast_clamp_fusion.2), kind=kCustom, calls=%fused_computation.clone.clone.1 | custom fusion | bytes 12288 | tf_op jit(solution)/shard_map/while/body/eval_jaxpr/jit(_take)/gather | solution.py:100
  111.1 0.8 compare_and_fusion.2
  112.0 2.9 %fusion.40 = (f32[8,512]{1,0:T(8,128)S(1)}, f32[1024,512,8]{1,0,2:T(8,128)S(1)}) fusion(pred[512,1024]{0,1:T(8,128)(4,1)S(1)} %compare_and_fusion.2, bf16[512,1,8,128]{3,0,2,1:T(8,128)(2,1)S(1)} %get-tuple-element.373, bf16[2048,128]{1,0:T(8,128)(2,1)S(1)} %get-tuple-element.372, s32[]{:T(128)S(6)} %select_n.145), kind=kOutput, calls=%fused_computation.5.clone.1 | convolution fusion | flops 1086320640 | bytes 18628612 | tf_op jit(solution)/shard_map/while/body/eval_jaxpr/rkgd,ckd->kgrc/dot_general | solution.py:27
  114.9 4.0 %fusion.42 = f32[8,512]{1,0:T(8,128)S(1)} fusion(f32[1024,512,8]{1,0,2:T(8,128)S(1)} %get-tuple-element.334, f32[8,512]{1,0:T(8,128)S(1)} %get-tuple-element.332, pred[512,1024]{0,1:T(8,128)(4,1)S(1)} %compare_and_fusion.2), kind=kLoop, calls=%fused_computation.7.clone.1 | loop fusion | flops 20967424 | bytes 17334272 | tf_op jit(solution)/shard_map/while/body/eval_jaxpr/reduce_sum | solution.py:34
  119.0 6.7 %bitcast_add_fusion.2 = f32[1,8,512,128]{3,2,1,0:T(8,128)} fusion(f32[1,8,512,128]{3,2,1,0:T(8,128)} %get-tuple-element.355, f32[1024,512,8]{1,0,2:T(8,128)S(1)} %get-tuple-element.334, f32[8,512]{1,0:T(8,128)S(1)} %get-tuple-element.332, pred[512,1024]{0,1:T(8,128)(4,1)S(1)} %compare_and_fusion.2, f32[8,512]{1,0:T(8,128)S(1)} %get-tuple-element.336, ...), kind=kOutput, calls=%fused_computation.11.clone.1 | convolution fusion | flops 1096810496 | bytes 21807108 | tf_op jit(solution)/shard_map/while/body/eval_jaxpr/kgrc,ckd->kgrd/dot_general | solution.py:35
  125.7 6.2 %gather_fusion = s32[1024]{0:T(1024)S(1)} fusion(s32[2048]{0:T(1024)S(1)} %get-tuple-element.370, s32[1024]{0:T(1024)S(1)} %broadcast_clamp_fusion.2), kind=kCustom, calls=%fused_computation.clone.clone.1 | custom fusion | bytes 12288 | tf_op jit(solution)/shard_map/while/body/eval_jaxpr/jit(_take)/gather | solution.py:100
  131.9 0.8 compare_and_fusion.2
  132.8 2.9 %fusion.40 = (f32[8,512]{1,0:T(8,128)S(1)}, f32[1024,512,8]{1,0,2:T(8,128)S(1)}) fusion(pred[512,1024]{0,1:T(8,128)(4,1)S(1)} %compare_and_fusion.2, bf16[512,1,8,128]{3,0,2,1:T(8,128)(2,1)S(1)} %get-tuple-element.373, bf16[2048,128]{1,0:T(8,128)(2,1)S(1)} %get-tuple-element.372, s32[]{:T(128)S(6)} %select_n.145), kind=kOutput, calls=%fused_computation.5.clone.1 | convolution fusion | flops 1086320640 | bytes 18628612 | tf_op jit(solution)/shard_map/while/body/eval_jaxpr/rkgd,ckd->kgrc/dot_general | solution.py:27
  135.7 4.0 %fusion.42 = f32[8,512]{1,0:T(8,128)S(1)} fusion(f32[1024,512,8]{1,0,2:T(8,128)S(1)} %get-tuple-element.334, f32[8,512]{1,0:T(8,128)S(1)} %get-tuple-element.332, pred[512,1024]{0,1:T(8,128)(4,1)S(1)} %compare_and_fusion.2), kind=kLoop, calls=%fused_computation.7.clone.1 | loop fusion | flops 20967424 | bytes 17334272 | tf_op jit(solution)/shard_map/while/body/eval_jaxpr/reduce_sum | solution.py:34
  139.8 7.7 %bitcast_add_fusion.2 = f32[1,8,512,128]{3,2,1,0:T(8,128)} fusion(f32[1,8,512,128]{3,2,1,0:T(8,128)} %get-tuple-element.355, f32[1024,512,8]{1,0,2:T(8,128)S(1)} %get-tuple-element.334, f32[8,512]{1,0:T(8,128)S(1)} %get-tuple-element.332, pred[512,1024]{0,1:T(8,128)(4,1)S(1)} %compare_and_fusion.2, f32[8,512]{1,0:T(8,128)S(1)} %get-tuple-element.336, ...), kind=kOutput, calls=%fused_computation.11.clone.1 | convolution fusion | flops 1096810496 | bytes 21807108 | tf_op jit(solution)/shard_map/while/body/eval_jaxpr/kgrc,ckd->kgrd/dot_general | solution.py:35
  147.5 2.0 %fusion.26 = bf16[512,1,8,128]{3,0,2,1:T(8,128)(2,1)S(1)} fusion(f32[1,8,512,128]{3,2,1,0:T(8,128)} %get-tuple-element.175, f32[8,512]{1,0:T(8,128)S(1)} %bitcast.131), kind=kLoop, calls=%fused_computation.42 | loop fusion | flops 1048576 | bytes 3162112 | tf_op jit(solution)/shard_map/convert_element_type | solution.py:110
  149.4 0.7 copy.16
  150.1 0.5 convert_element_type.19
  150.6 30.0 %all_to_all.56 = bf16[8,64,1024]{2,1,0:T(8,128)(2,1)S(1)} all-to-all(bf16[8,64,1024]{2,1,0:T(8,128)(2,1)S(1)} %convert_element_type.19), channel_id=1, replica_groups=mesh['head'=8,'kv'=4] {'head'}, dimensions={0} | all-to-all | bytes 2097152 | tf_op jit(solution)/shard_map/all_to_all | solution.py:111
  180.6 1.1 copy.21
  (21 shorter events, 0.2 us)
Async XLA Ops:
  0.0 0.9 copy-start
  1.6 16.9 %all-to-all-start = ((bf16[64,8,128]{2,0,1:T(8,128)(2,1)}), bf16[64,8,128]{2,0,1:T(8,128)(2,1)S(1)}, u32[]{:S(2)}, u32[]{:S(2)}) async-start(bf16[64,8,128]{2,0,1:T(8,128)(2,1)} %copy_bitcast_fusion.1), calls=%async_computation | async-start | bytes 262144 | tf_op jit(solution)/shard_map/all_to_all | solution.py:66
  18.5 11.8 %all-to-all-start.2 = ((bf16[8,64,128]{2,1,0:T(8,128)(2,1)}), bf16[8,64,128]{2,1,0:T(8,128)(2,1)S(1)}, u32[]{:S(2)}, u32[]{:S(2)}) async-start(bf16[8,64,128]{2,1,0:T(8,128)(2,1)} %constant_dynamic-update-slice_fusion), calls=%async_computation.2 | async-start | bytes 262144 | tf_op jit(solution)/shard_map/all_to_all | solution.py:68
  30.3 74.1 %all-to-all-start.1 = ((bf16[64,8,1024]{2,0,1:T(8,128)(2,1)}), bf16[64,8,1024]{2,0,1:T(8,128)(2,1)S(1)}, u32[]{:S(2)}, u32[]{:S(2)}) async-start(bf16[64,8,1024]{2,0,1:T(8,128)(2,1)} %bitcast.102), calls=%async_computation.1 | async-start | bytes 2097152 | tf_op jit(solution)/shard_map/all_to_all | solution.py:65
